TPU v7x, 32 devices: a whole 2x2x4 slice. The times are simulated.
32 devices in a mesh: rows: 8 (over z, x), cols: 4 (over y, core).
Axes of the slice: x: 2, y: 2, z: 4, core: 2. Of those that a mesh axis runs over, the one named last changes fastest.
Arguments:
- panel: float32 [4096, 1024], P('rows'), as said below
- window_block: float32 [4096, 2048], P('rows', 'cols'), may hold values from -6 to 6
- row_live: int32 [8], replicated, may hold values 0 or 1
- window_rows: int32 [4], replicated, may hold values from 2 to 7, as said below
Outputs:
- factor: float32 [4096, 1024], P('rows')
- updated: float32 [4096, 2048], P('rows', 'cols')
Inputs may be any that keep to these rules, and one draw needn't show every extreme that they name: `window_rows`: distinct tile rows, none inside the supernode. `row_live`: the value for tile rows below 2 is ignored: those rows are always present. `panel`: the first 1024 rows hold a symmetric positive definite block.
All inputs are finite; a program needn't handle non-finite values.
Results may differ from a plain program's by a relative error of at most 0.0001.
Values sent between devices are 32-bit elements; how exact they have to be, the bound alone decides.
A program may use at most 128 MiB of HBM per device.

v0:
```python
import jax
import jax.numpy as jnp
from jax import lax
from jax.sharding import PartitionSpec as P

P_SIZE = 2
HIGHEST = lax.Precision.HIGHEST
CONTRACT = (((1,), (1,)), ((), ()))


def from_root(value, axis, source):
    kept = jnp.where(lax.axis_index(axis) == source, value, 0).astype(value.dtype)
    return lax.psum(kept, axis)


def times_trans(left, right):
    return lax.dot_general(left, right, CONTRACT, precision=HIGHEST)


def symmetric(square):
    return jnp.tril(square) + jnp.tril(square, -1).T


def factor_tile(square):
    lower_tile = jnp.linalg.cholesky(square)
    identity_tile = jnp.eye(square.shape[0], dtype=jnp.float32)
    inverse = lax.linalg.triangular_solve(lower_tile, identity_tile, left_side=True, lower=True)
    return (lower_tile, inverse)


def column(block, section, width):
    return block[:, section * width : (section + 1) * width]


def solve_row(block, super_rows, inverses, width):
    tiles_now = []
    for section in range(P_SIZE):
        update = column(block, section, width)
        for earlier in range(section):
            update = update - times_trans(tiles_now[earlier], super_rows[section][earlier])
        tiles_now.append(times_trans(update, inverses[section]))
    return jnp.concatenate(tiles_now, axis=1)


def shards(panel, window_block, row_live, window_rows):
    width = panel.shape[0]
    device_row = lax.axis_index("rows")
    device_col = lax.axis_index("cols")
    live_flag = jnp.where(device_row < P_SIZE, 1, row_live[device_row]).astype(jnp.float32)
    scaled = panel * live_flag
    target = window_rows[device_col]
    target_raw = from_root(scaled, "rows", target)
    own_tiles = []
    super_rows = []
    inverses = []
    identity_tile = jnp.eye(width, dtype=jnp.float32)
    for section in range(P_SIZE):
        square = symmetric(column(scaled, section, width))
        for earlier in range(section):
            square = square - times_trans(own_tiles[earlier], own_tiles[earlier])
        square = jnp.where(device_row == section, square, identity_tile)
        lower_tile, inverse = factor_tile(square)
        payload = jnp.concatenate(own_tiles + [inverse], axis=1)
        received = from_root(payload, "rows", section)
        earlier_tiles = [column(received, earlier, width) for earlier in range(section)]
        inverses.append(column(received, section, width))
        super_rows.append(earlier_tiles)
        update = column(scaled, section, width)
        for earlier in range(section):
            update = update - times_trans(own_tiles[earlier], earlier_tiles[earlier])
        solved = times_trans(update, inverses[section])
        solved = jnp.where(device_row == section, lower_tile, solved)
        solved = jnp.where(device_row < section, jnp.zeros_like(solved), solved)
        own_tiles.append(solved)
    own_row = jnp.concatenate(own_tiles, axis=1)
    target_row = solve_row(target_raw, super_rows, inverses, width)
    updated = window_block - times_trans(own_row, target_row)
    return (own_row, updated)


def solution(mesh):
    in_specs = (P("rows", None), P("rows", "cols"), P(), P())
    out_specs = (P("rows", None), P("rows", "cols"))
    return jax.shard_map(shards, mesh=mesh, in_specs=in_specs, out_specs=out_specs, check_vma=False)
```

profile of v0, /device:TPU:0, one launch (start us, length us, event | category | flops | bytes accessed | tf_op | source)
XLA Modules:
  0.0 616.2 jit_solution(17323084982662087415)
XLA Ops:
  12.1 3.6 broadcast_select_fusion
  23.6 11.7 %cholesky.286 = f32[128,128]{1,0:T(8,128)S(1)} custom-call(f32[128,128]{1,0:T(8,128)S(1)} %cholesky.426), custom_call_target="Cholesky" | custom-call | tf_op jit(solution)/shard_map/jit(cholesky)/cholesky | solution.py:25
  35.9 9.8 %custom-call.27 = f32[1,128,128]{1,2,0:T(8,128)S(1)} custom-call(f32[1,128,128]{2,1,0:T(8,128)S(1)} %get-tuple-element.65), custom_call_target="InvertDiagBlocksLowerTriangular" | custom-call | tf_op jit(solution)/shard_map/jit(cholesky)/cholesky | solution.py:25
  48.6 12.5 %cholesky.305 = f32[128,128]{1,0:T(8,128)} custom-call(f32[128,128]{1,0:T(8,128)S(1)} %cholesky.430), custom_call_target="Cholesky" | custom-call | tf_op jit(solution)/shard_map/jit(cholesky)/cholesky | solution.py:25
  63.0 9.8 %custom-call.28 = f32[1,128,128]{1,2,0:T(8,128)S(1)} custom-call(f32[1,128,128]{2,1,0:T(8,128)S(1)} %get-tuple-element.62), custom_call_target="InvertDiagBlocksLowerTriangular" | custom-call | tf_op jit(solution)/shard_map/jit(cholesky)/cholesky | solution.py:25
  74.4 11.7 %cholesky.326 = f32[128,128]{1,0:T(8,128)S(1)} custom-call(f32[128,128]{1,0:T(8,128)S(1)} %cholesky.435), custom_call_target="Cholesky" | custom-call | tf_op jit(solution)/shard_map/jit(cholesky)/cholesky | solution.py:25
  86.8 9.8 %custom-call.29 = f32[1,128,128]{1,2,0:T(8,128)S(1)} custom-call(f32[1,128,128]{2,1,0:T(8,128)S(1)} %get-tuple-element.59), custom_call_target="InvertDiagBlocksLowerTriangular" | custom-call | tf_op jit(solution)/shard_map/jit(cholesky)/cholesky | solution.py:25
  98.0 11.9 %cholesky.343 = f32[128,128]{1,0:T(8,128)S(1)} custom-call(f32[128,128]{1,0:T(8,128)S(1)} %convolution_subtract_fusion.14), custom_call_target="Cholesky" | custom-call | tf_op jit(solution)/shard_map/jit(cholesky)/cholesky | solution.py:25
  115.1 11.9 %while.4 = (s32[]{:T(128)}, f32[512,512]{1,0:T(8,128)}, s32[4,2]{0,1:T(2,128)S(1)}, f32[4,128,128]{2,1,0:T(8,128)S(1)}, s32[]{:T(128)}) while((s32[]{:T(128)}, f32[512,512]{1,0:T(8,128)}, s32[4,2]{0,1:T(2,128)S(1)}, f32[4,128,128]{2,1,0:T(8,128)S(1)}, s32[]{:T(128)}) %tuple.55), condition=%wide.while_cond, body=%wide.while_body.sunk | while | flops 2 | bytes 131189 | solution.py:27
  115.8 2.3 bitcast_dynamic-update-slice_fusion.4
  118.8 2.3 bitcast_dynamic-update-slice_fusion.4
  121.8 2.3 bitcast_dynamic-update-slice_fusion.4
  124.8 2.2 bitcast_dynamic-update-slice_fusion.4
  127.7 40.1 %custom-call.30 = f32[4,128,128]{1,2,0:T(8,128)S(1)} custom-call(f32[4,128,128]{2,1,0:T(8,128)} %copy-done.15), custom_call_target="InvertDiagBlocksLowerTriangular" | custom-call | tf_op jit(solution)/shard_map/triangular_solve/custom-call.3 | solution.py:27
  169.3 1.6 convolution_subtract_fusion.6
  171.4 1.9 convolution_subtract_fusion.5
  173.7 2.4 convolution_subtract_fusion.8
  179.5 79.4 %all-reduce.5.cloned.1.call-done = f32[512,512]{1,0:T(8,128)} async-done(((f32[512,512]{1,0:T(8,128)}), f32[512,512]{1,0:T(8,128)}) %all-reduce.5.cloned.1.call-update) | async-done | bytes 1048592 | tf_op jit(solution)/shard_map/psum | solution.py:13
  258.9 3.6 fusion.10
  262.6 2.9 fusion.8
  265.5 2.6 copy.19
  268.1 1.8 fusion.13
  270.9 11.7 %cholesky.358 = f32[128,128]{1,0:T(8,128)S(1)} custom-call(f32[128,128]{1,0:T(8,128)S(1)} %cholesky.439), custom_call_target="Cholesky" | custom-call | tf_op jit(solution)/shard_map/jit(cholesky)/cholesky | solution.py:25
  283.2 9.8 %custom-call.31 = f32[1,128,128]{1,2,0:T(8,128)S(1)} custom-call(f32[1,128,128]{2,1,0:T(8,128)S(1)} %get-tuple-element.55), custom_call_target="InvertDiagBlocksLowerTriangular" | custom-call | tf_op jit(solution)/shard_map/jit(cholesky)/cholesky | solution.py:25
  294.3 2.1 convolution_subtract_fusion.9
  298.1 11.9 %cholesky.377 = f32[128,128]{1,0:T(8,128)S(1)} custom-call(f32[128,128]{1,0:T(8,128)S(1)} %cholesky.443), custom_call_target="Cholesky" | custom-call | tf_op jit(solution)/shard_map/jit(cholesky)/cholesky | solution.py:25
  310.0 1.9 cholesky.384
  313.9 9.8 %custom-call.32 = f32[1,128,128]{1,2,0:T(8,128)S(1)} custom-call(f32[1,128,128]{2,1,0:T(8,128)S(1)} %get-tuple-element.52), custom_call_target="InvertDiagBlocksLowerTriangular" | custom-call | tf_op jit(solution)/shard_map/jit(cholesky)/cholesky | solution.py:25
  323.7 1.8 convolution_dynamic-update-slice_fusion
  327.0 11.7 %cholesky.398 = f32[128,128]{1,0:T(8,128)S(1)} custom-call(f32[128,128]{1,0:T(8,128)S(1)} %cholesky.448), custom_call_target="Cholesky" | custom-call | tf_op jit(solution)/shard_map/jit(cholesky)/cholesky | solution.py:25
  340.1 10.0 %custom-call.33 = f32[1,128,128]{1,2,0:T(8,128)S(1)} custom-call(f32[1,128,128]{2,1,0:T(8,128)S(1)} %get-tuple-element.49), custom_call_target="InvertDiagBlocksLowerTriangular" | custom-call | tf_op jit(solution)/shard_map/jit(cholesky)/cholesky | solution.py:25
  352.3 11.7 %cholesky.415 = f32[128,128]{1,0:T(8,128)S(1)} custom-call(f32[128,128]{1,0:T(8,128)S(1)} %convolution_subtract_fusion.13), custom_call_target="Cholesky" | custom-call | tf_op jit(solution)/shard_map/jit(cholesky)/cholesky | solution.py:25
  367.8 2.4 fusion.16
  370.2 11.7 %while.5 = (s32[]{:T(128)}, f32[512,512]{1,0:T(8,128)}, s32[4,2]{0,1:T(2,128)S(1)}, f32[4,128,128]{2,1,0:T(8,128)S(1)}, s32[]{:T(128)}) while((s32[]{:T(128)}, f32[512,512]{1,0:T(8,128)}, s32[4,2]{0,1:T(2,128)S(1)}, f32[4,128,128]{2,1,0:T(8,128)S(1)}, s32[]{:T(128)}) %tuple.66), condition=%wide.while_cond.clone, body=%wide.while_body.clone.sunk | while | flops 2 | bytes 131189 | solution.py:27
  370.9 2.3 bitcast_dynamic-update-slice_fusion.5
  373.8 2.3 bitcast_dynamic-update-slice_fusion.5
  376.7 2.3 bitcast_dynamic-update-slice_fusion.5
  379.7 2.2 bitcast_dynamic-update-slice_fusion.5
  382.6 40.5 %custom-call.34 = f32[4,128,128]{1,2,0:T(8,128)S(1)} custom-call(f32[4,128,128]{2,1,0:T(8,128)} %copy-done.14), custom_call_target="InvertDiagBlocksLowerTriangular" | custom-call | tf_op jit(solution)/shard_map/triangular_solve/custom-call.3 | solution.py:27
  426.6 1.9 convolution_subtract_fusion.3
  429.0 2.4 convolution_subtract_fusion.7
  433.4 156.2 %all-reduce.7.cloned.1.call-done = (f32[512,1024]{1,0:T(8,128)}, f32[512,1024]{1,0:T(8,128)}) async-done(((f32[512,1024]{1,0:T(8,128)}, f32[512,1024]{1,0:T(8,128)}), (f32[512,1024]{1,0:T(8,128)}, f32[512,1024]{1,0:T(8,128)})) %all-reduce.7.cloned.1.call-update) | async-done | bytes 4194320 | tf_op jit(solution)/shard_map/psum | solution.py:13
  589.5 3.2 convolution_subtract_fusion.1
  592.8 1.9 fusion.11
  594.7 3.5 convolution_subtract_fusion
  598.2 2.1 fusion.19
  600.2 3.2 fusion.9
  604.7 4.5 fusion.5
  (115 shorter events, 55.6 us)
Async XLA Ops:
  7.2 251.8 %all-reduce.5.cloned.1.call-start = ((), (), s32[]{:S(2)}) async-start(), calls=%async_computation | async-start | bytes 2097152 | tf_op jit(solution)/shard_map/psum | solution.py:13
  22.6 1.0 copy-start.9
  35.3 0.6 copy-start.13
  110.0 61.0 %copy-start = (f32[512,512]{1,0:T(8,128)}, f32[512,512]{1,0:T(8,128)S(1)}, u32[]{:S(2)}) copy-start(f32[512,512]{1,0:T(8,128)S(1)} %get-tuple-element.57) | copy-start | bytes 3145732
  127.0 0.7 copy-start.15
  167.9 3.5 copy-start.1
  176.1 2.0 copy-start.7
  177.7 411.9 %all-reduce.7.cloned.1.call-start = ((), (), s32[]{:S(2)}) async-start(), calls=%async_computation.1 | async-start | bytes 8388608 | tf_op jit(solution)/shard_map/psum | solution.py:13
  258.9 3.6 copy-start.6
  269.9 1.0 copy-start.8
  282.6 0.6 copy-start.12
  381.9 0.7 copy-start.14
  423.1 3.5 copy-start.2
  589.5 3.2 copy-start.5
  589.5 3.3 copy-start.10
  592.8 1.9 copy-start.4
  603.5 1.2 copy-start.11
  604.7 4.5 copy-start.3
Sparse Core Ops, SparseCore 0:
  177.8 81.0 all-reduce.4
  433.5 156.0 all-reduce.6
where the time goes:
time: 626 us; the launch traced here: 616 us
  other arithmetic  258 us (41%)
  waiting for transfers between devices  236 us (38%)
  matrix products  56.8 us (9%)
  local copies, waits for them, and re-layouts  44.3 us (7%)
  between operations  21 us (3%)
    psum x2, waiting for transfers between devices, from_root(): return lax.psum(kept, axis)  236 us
    another operation x29, other arithmetic, factor_tile(): lower_tile = jnp.linalg.cholesky(square)  162 us
    another operation x5, other arithmetic, factor_tile(): lax.linalg.triangular_solve(lower_tile, identity_tile, left_side=True, lo...  84.1 us
    dot_general x8, matrix products, times_trans(): return lax.dot_general(left, right, CONTRACT, precision=HIGHEST)  24.9 us
    another operation x27, local copies, waits for them, and re-layouts, factor_tile(): lax.linalg.triangular_solve(lower_tile, identity_tile, left_side=True, lo...  23.5 us
    another operation x14, matrix products, factor_tile(): lax.linalg.triangular_solve(lower_tile, identity_tile, left_side=True, lo...  17.2 us
    another operation x12, matrix products, factor_tile(): lower_tile = jnp.linalg.cholesky(square)  14.7 us
  transfers between devices with their start and end apart: 2, of which 2 were waited for; matrix products, arithmetic and copies ran while one was open for 0% of the time, Pallas kernels for 0%

commit v1 on v0

--- a/solution.py
+++ b/solution.py
@@ -10,7 +10,7 @@
 
 def from_root(value, axis, source):
     kept = jnp.where(lax.axis_index(axis) == source, value, 0).astype(value.dtype)
-    return lax.psum(kept, axis)
+    return jnp.sum(lax.all_gather(kept, axis_name=axis), 0)
 
 
 def times_trans(left, right):

time: 626 us -> 810 us (1.29)
  waiting for transfers between devices: 236 us -> 371 us
  other arithmetic: 258 us -> 281 us
  local copies, waits for them, and re-layouts: 44.3 us -> 66.6 us
    all_gather x0 -> x3, waiting for transfers between devices: none -> 370 us  [from_root(): return jnp.sum(lax.all_gather(kept, axis_name=axis), 0)]
    psum x2 -> x0, waiting for transfers between devices: 236 us -> none  [from_root(): return lax.psum(kept, axis)]
    unnamed x33 -> x38, local copies, waits for them, and re-layouts: 7.05 us -> 29.9 us
    reduce_sum x0 -> x3, other arithmetic: none -> 21.6 us  [from_root(): return jnp.sum(lax.all_gather(kept, axis_name=axis), 0)]
  transfers between devices with their start and end apart: 2 -> 3, of which waited for: 2 -> 3; matrix products, arithmetic and copies ran while one was open for 0% -> 26% of each run, Pallas kernels for 0% -> 0%
where the time goes in v1:
time: 810 us; the launch traced here: 799 us
  waiting for transfers between devices  371 us (46%)
  other arithmetic  281 us (35%)
  local copies, waits for them, and re-layouts  66.6 us (8%)
  matrix products  59.8 us (7%)
  between operations  21.1 us (3%)
    all_gather x3, waiting for transfers between devices, from_root(): return jnp.sum(lax.all_gather(kept, axis_name=axis), 0)  370 us
    another operation x29, other arithmetic, factor_tile(): lower_tile = jnp.linalg.cholesky(square)  162 us
    another operation x5, other arithmetic, factor_tile(): lax.linalg.triangular_solve(lower_tile, identity_tile, left_side=True, lo...  83.7 us
    unnamed x38, local copies, waits for them, and re-layouts  29.9 us
    dot_general x8, matrix products, times_trans(): return lax.dot_general(left, right, CONTRACT, precision=HIGHEST)  28.6 us
    another operation x27, local copies, waits for them, and re-layouts, factor_tile(): lax.linalg.triangular_solve(lower_tile, identity_tile, left_side=True, lo...  23.4 us
    reduce_sum x3, other arithmetic, from_root(): return jnp.sum(lax.all_gather(kept, axis_name=axis), 0)  21.6 us
    another operation x14, matrix products, factor_tile(): lax.linalg.triangular_solve(lower_tile, identity_tile, left_side=True, lo...  17.3 us
  transfers between devices with their start and end apart: 3, of which 3 were waited for; matrix products, arithmetic and copies ran while one was open for 26% of the time, Pallas kernels for 0%

profile of v1, /device:TPU:0, one launch (start us, length us, event | category | flops | bytes accessed | tf_op | source)
XLA Modules:
  0.0 799.3 jit_solution(14086614450274021821)
XLA Ops:
  12.1 2.9 copy.24
  15.0 3.5 broadcast_select_fusion
  19.9 2.5 fusion.85
  26.2 11.7 %cholesky.286 = f32[128,128]{1,0:T(8,128)S(1)} custom-call(f32[128,128]{1,0:T(8,128)S(1)} %cholesky.426), custom_call_target="Cholesky" | custom-call | tf_op jit(solution)/shard_map/jit(cholesky)/cholesky | solution.py:25
  38.6 9.8 %custom-call.27 = f32[1,128,128]{1,2,0:T(8,128)S(1)} custom-call(f32[1,128,128]{2,1,0:T(8,128)S(1)} %get-tuple-element.63), custom_call_target="InvertDiagBlocksLowerTriangular" | custom-call | tf_op jit(solution)/shard_map/jit(cholesky)/cholesky | solution.py:25
  51.3 12.3 %cholesky.305 = f32[128,128]{1,0:T(8,128)} custom-call(f32[128,128]{1,0:T(8,128)S(1)} %cholesky.430), custom_call_target="Cholesky" | custom-call | tf_op jit(solution)/shard_map/jit(cholesky)/cholesky | solution.py:25
  65.7 9.8 %custom-call.28 = f32[1,128,128]{1,2,0:T(8,128)S(1)} custom-call(f32[1,128,128]{2,1,0:T(8,128)S(1)} %get-tuple-element.60), custom_call_target="InvertDiagBlocksLowerTriangular" | custom-call | tf_op jit(solution)/shard_map/jit(cholesky)/cholesky | solution.py:25
  77.1 11.7 %cholesky.326 = f32[128,128]{1,0:T(8,128)S(1)} custom-call(f32[128,128]{1,0:T(8,128)S(1)} %cholesky.435), custom_call_target="Cholesky" | custom-call | tf_op jit(solution)/shard_map/jit(cholesky)/cholesky | solution.py:25
  89.5 9.8 %custom-call.29 = f32[1,128,128]{1,2,0:T(8,128)S(1)} custom-call(f32[1,128,128]{2,1,0:T(8,128)S(1)} %get-tuple-element.57), custom_call_target="InvertDiagBlocksLowerTriangular" | custom-call | tf_op jit(solution)/shard_map/jit(cholesky)/cholesky | solution.py:25
  100.8 12.1 %cholesky.343 = f32[128,128]{1,0:T(8,128)S(1)} custom-call(f32[128,128]{1,0:T(8,128)S(1)} %convolution_subtract_fusion.14), custom_call_target="Cholesky" | custom-call | tf_op jit(solution)/shard_map/jit(cholesky)/cholesky | solution.py:25
  118.2 11.9 %while.4 = (s32[]{:T(128)}, f32[512,512]{1,0:T(8,128)}, s32[4,2]{0,1:T(2,128)S(1)}, f32[4,128,128]{2,1,0:T(8,128)S(1)}, s32[]{:T(128)}) while((s32[]{:T(128)}, f32[512,512]{1,0:T(8,128)}, s32[4,2]{0,1:T(2,128)S(1)}, f32[4,128,128]{2,1,0:T(8,128)S(1)}, s32[]{:T(128)}) %tuple.55), condition=%wide.while_cond, body=%wide.while_body.sunk | while | flops 2 | bytes 131189 | solution.py:27
  118.9 2.3 bitcast_dynamic-update-slice_fusion.4
  121.9 2.3 bitcast_dynamic-update-slice_fusion.4
  124.9 2.3 bitcast_dynamic-update-slice_fusion.4
  127.9 2.2 bitcast_dynamic-update-slice_fusion.4
  130.9 40.1 %custom-call.30 = f32[4,128,128]{1,2,0:T(8,128)S(1)} custom-call(f32[4,128,128]{2,1,0:T(8,128)} %copy-done.16), custom_call_target="InvertDiagBlocksLowerTriangular" | custom-call | tf_op jit(solution)/shard_map/triangular_solve/custom-call.3 | solution.py:27
  176.9 2.4 convolution_subtract_fusion.8
  183.4 124.8 %all-gather.8.cloned.1.call-done = f32[4096,512]{1,0:T(8,128)} async-done(((f32[512,512]{1,0:T(8,128)}), f32[4096,512]{1,0:T(8,128)}) %all-gather.8.cloned.1.call-update) | async-done | bytes 8388624 | tf_op jit(solution)/shard_map/all_gather | solution.py:13
  308.2 5.5 reduce_sum.27
  313.6 5.1 fusion.9
  318.8 3.0 fusion.7
  321.7 2.6 copy.37
  327.1 11.7 %cholesky.358 = f32[128,128]{1,0:T(8,128)S(1)} custom-call(f32[128,128]{1,0:T(8,128)S(1)} %cholesky.439), custom_call_target="Cholesky" | custom-call | tf_op jit(solution)/shard_map/jit(cholesky)/cholesky | solution.py:25
  339.4 10.0 %custom-call.31 = f32[1,128,128]{1,2,0:T(8,128)S(1)} custom-call(f32[1,128,128]{2,1,0:T(8,128)S(1)} %get-tuple-element.53), custom_call_target="InvertDiagBlocksLowerTriangular" | custom-call | tf_op jit(solution)/shard_map/jit(cholesky)/cholesky | solution.py:25
  353.0 11.7 %cholesky.377 = f32[128,128]{1,0:T(8,128)S(1)} custom-call(f32[128,128]{1,0:T(8,128)S(1)} %cholesky.443), custom_call_target="Cholesky" | custom-call | tf_op jit(solution)/shard_map/jit(cholesky)/cholesky | solution.py:25
  364.7 2.0 cholesky.384
  368.0 9.8 %custom-call.32 = f32[1,128,128]{1,2,0:T(8,128)S(1)} custom-call(f32[1,128,128]{2,1,0:T(8,128)S(1)} %get-tuple-element.50), custom_call_target="InvertDiagBlocksLowerTriangular" | custom-call | tf_op jit(solution)/shard_map/jit(cholesky)/cholesky | solution.py:25
  381.2 12.1 %cholesky.398 = f32[128,128]{1,0:T(8,128)S(1)} custom-call(f32[128,128]{1,0:T(8,128)S(1)} %cholesky.448), custom_call_target="Cholesky" | custom-call | tf_op jit(solution)/shard_map/jit(cholesky)/cholesky | solution.py:25
  393.9 9.8 %custom-call.33 = f32[1,128,128]{1,2,0:T(8,128)S(1)} custom-call(f32[1,128,128]{2,1,0:T(8,128)S(1)} %get-tuple-element.47), custom_call_target="InvertDiagBlocksLowerTriangular" | custom-call | tf_op jit(solution)/shard_map/jit(cholesky)/cholesky | solution.py:25
  406.0 11.7 %cholesky.415 = f32[128,128]{1,0:T(8,128)S(1)} custom-call(f32[128,128]{1,0:T(8,128)S(1)} %convolution_subtract_fusion.13), custom_call_target="Cholesky" | custom-call | tf_op jit(solution)/shard_map/jit(cholesky)/cholesky | solution.py:25
  423.5 2.4 fusion.15
  425.9 11.8 %while.5 = (s32[]{:T(128)}, f32[512,512]{1,0:T(8,128)}, s32[4,2]{0,1:T(2,128)S(1)}, f32[4,128,128]{2,1,0:T(8,128)S(1)}, s32[]{:T(128)}) while((s32[]{:T(128)}, f32[512,512]{1,0:T(8,128)}, s32[4,2]{0,1:T(2,128)S(1)}, f32[4,128,128]{2,1,0:T(8,128)S(1)}, s32[]{:T(128)}) %tuple.67), condition=%wide.while_cond.clone, body=%wide.while_body.clone.sunk | while | flops 2 | bytes 131189 | solution.py:27
  426.7 2.2 bitcast_dynamic-update-slice_fusion.5
  429.6 2.2 bitcast_dynamic-update-slice_fusion.5
  432.6 2.2 bitcast_dynamic-update-slice_fusion.5
  435.5 2.2 bitcast_dynamic-update-slice_fusion.5
  438.4 40.1 %custom-call.34 = f32[4,128,128]{1,2,0:T(8,128)S(1)} custom-call(f32[4,128,128]{2,1,0:T(8,128)} %copy-done.17), custom_call_target="InvertDiagBlocksLowerTriangular" | custom-call | tf_op jit(solution)/shard_map/triangular_solve/custom-call.3 | solution.py:27
  484.4 2.4 convolution_subtract_fusion.7
  488.8 47.6 %all-gather.10.cloned.1.call-done = f32[4096,1024]{0,1:T(8,128)} async-done(((f32[512,1024]{0,1:T(8,128)}), f32[4096,1024]{0,1:T(8,128)}) %all-gather.10.cloned.1.call-update) | async-done | bytes 16777232 | tf_op jit(solution)/shard_map/all_gather | solution.py:13
  536.4 19.1 %copy.62 = f32[128,8,8,512]{3,2,1,0:T(8,128)S(1)} copy(f32[128,8,8,512]{3,1,2,0:T(8,128)} %bitcast.121) | data formatting | bytes 33554432
  555.6 6.9 bitcast_reduce_fusion
  563.9 2.8 fusion.10
  566.7 197.4 %all-gather.6.cloned.1.call-done = f32[8,512,1024]{2,1,0:T(8,128)} async-done(((f32[1,512,1024]{2,1,0:T(8,128)}), f32[8,512,1024]{2,1,0:T(8,128)}) %all-gather.6.cloned.1.call-update) | async-done | bytes 16777232 | tf_op jit(solution)/shard_map/all_gather | solution.py:13
  764.1 9.3 %reduce_sum.28 = f32[512,1024]{1,0:T(8,128)} reduce(f32[8,512,1024]{2,1,0:T(8,128)} %all-gather.6.cloned.1.call-done, f32[]{:T(128)} %constant.127.clone.1), dimensions={0}, to_apply=%region_9.12 | reduce | flops 3670016 | bytes 18874372 | tf_op jit(solution)/shard_map/reduce_sum | solution.py:13
  773.4 3.2 convolution_subtract_fusion.1
  776.6 3.1 convolution_subtract_fusion
  781.6 5.0 fusion.8
  787.8 4.5 fusion.4
  (128 shorter events, 67.4 us)
Async XLA Ops:
  7.2 301.0 %all-gather.8.cloned.1.call-start = ((), (), s32[]{:S(2)}) async-start(), calls=%async_computation.1 | async-start | bytes 9437184 | tf_op jit(solution)/shard_map/all_gather | solution.py:13
  25.2 1.0 copy-start.10
  37.9 0.6 copy-start.14
  112.9 61.2 %copy-start.1 = (f32[512,512]{1,0:T(8,128)}, f32[512,512]{1,0:T(8,128)S(1)}, u32[]{:S(2)}) copy-start(f32[512,512]{1,0:T(8,128)S(1)} %get-tuple-element.55) | copy-start | bytes 3145732
  130.2 0.7 copy-start.16
  171.0 3.5 copy-start.3
  180.8 1.2 copy-start.8
  180.8 355.6 %all-gather.10.cloned.1.call-start = ((), (), s32[]{:S(2)}) async-start(), calls=%async_computation.2 | async-start | bytes 18874368 | tf_op jit(solution)/shard_map/all_gather | solution.py:13
  181.6 582.5 %all-gather.6.cloned.1.call-start = ((), (), s32[]{:S(2)}) async-start(), calls=%async_computation | async-start | bytes 18874368 | tf_op jit(solution)/shard_map/all_gather | solution.py:13
  313.6 5.1 copy-start.9
  326.1 1.0 copy-start.11
  338.8 0.6 copy-start.15
  352.3 0.7 copy-start.13
  437.7 0.7 copy-start.17
  478.5 3.5 copy-start.4
  555.6 8.3 %copy-start.2 = (f32[512,512]{1,0:T(8,128)S(1)}, f32[512,512]{1,0:T(8,128)}, u32[]{:S(2)}) copy-start(f32[512,512]{1,0:T(8,128)} %reduce_sum.27) | copy-start | bytes 3145732
  562.5 1.4 copy-start.6
  773.4 3.2 copy-start
  773.4 3.3 copy-start.5
  786.6 1.2 copy-start.12
  787.8 4.5 copy-start.7
Sparse Core Ops, SparseCore 0:
  181.0 127.1 all-gather.7
  310.9 225.4 all-gather.9
  538.6 225.4 all-gather.5
